TPU v7x, 32 devices: a whole 2x2x4 slice. The times are simulated.
32 devices in a mesh: level: 2 (over core), gx: 4 (over y, x), yz: 4 (over z).
Axes of the slice: x: 2, y: 2, z: 4, core: 2. Of those that a mesh axis runs over, the one named last changes fastest.
Arguments:
- init_field: float32 [128, 64, 256], P('gx', 'yz'), may hold values from -6 to 6
- source: float32 [128, 64, 256], P('gx', 'yz'), may hold values from -4 to 4
- damping: float32 [128, 64, 256], P('gx', 'yz'), may hold values from 0.05 to 2
Outputs:
- final_states: float32 [2, 128, 64, 256], P('level', 'gx', 'yz')
All inputs are finite; a program needn't handle non-finite values.
Results may differ from a plain program's by a relative error of at most 0.0001.
Values sent between devices are 32-bit elements; how exact they have to be, the bound alone decides.
A program may use at most 64 MiB of HBM per device.

v0:
```python
import jax
import jax.numpy as jnp
from jax import lax
from jax.sharding import PartitionSpec as P

STEPS = 3
ITERS = 3
diffusion_number = 1.0


def extended(cells, sides, width):
    for axis, dim in sides:
        count = lax.axis_size(axis)
        ends = count - 1
        head = lax.slice_in_dim(cells, 0, width, axis=dim)
        tail = lax.slice_in_dim(cells, cells.shape[dim] - width, cells.shape[dim], axis=dim)
        cells = jnp.concatenate(
            [
                lax.ppermute(tail, axis, [(i, (i + 1) % count) for i in range(ends)]),
                cells,
                lax.ppermute(head, axis, [((i + 1) % count, i) for i in range(ends)]),
            ],
            axis=dim,
        )
    return cells


def passed_along(block, axis, distance):
    devices = range(lax.axis_size(axis))
    route = [(i - distance, i) for i in devices if i - distance in devices]
    return lax.ppermute(block, axis, route)


def stencil_from(padded, field, damping):
    beside = padded[2:, 1:-1, :] + padded[:-2, 1:-1, :]
    beside = beside + padded[1:-1, 2:, :] + padded[1:-1, :-2, :]
    zero_plane = jnp.zeros_like(field[:, :, :1])
    beside = beside + jnp.concatenate([field[:, :, 1:], zero_plane], axis=2)
    beside = beside + jnp.concatenate([zero_plane, field[:, :, :-1]], axis=2)
    return damping * field + diffusion_number * (6.0 * field - beside)


def operate(field, damping):
    padded = extended(field, (("gx", 0), ("yz", 1)), 1)
    return field + stencil_from(padded, field, damping)


def two_products(resid, image):
    return lax.psum((jnp.sum(resid * resid), jnp.sum(resid * image)), ("gx", "yz"))


def solve(target, guess, damping):
    answer = guess
    resid = target - operate(answer, damping)
    image = operate(resid, damping)
    norm_now, product = two_products(resid, image)
    alpha = norm_now / product
    direction, along = (resid, image)
    for step in range(ITERS):
        answer = answer + alpha * direction
        resid = resid - alpha * along
        if step + 1 < ITERS:
            image = operate(resid, damping)
            norm_next, product = two_products(resid, image)
            ratio = norm_next / norm_now
            alpha = norm_next / (product - ratio * norm_next / alpha)
            direction = resid + ratio * direction
            along = image + ratio * along
            norm_now = norm_next
    return answer


def per_device(init_field, source, damping):
    upper = lax.axis_index("level") == 1
    state = init_field
    older = jnp.where(upper, init_field, jnp.zeros_like(init_field))
    for rounds in range(STEPS + 1):
        if rounds == 0:
            extra = jnp.zeros_like(init_field)
        else:
            incoming = passed_along(state, "level", 1)
            change = incoming - older
            older = incoming
            padded = extended(change, (("gx", 0), ("yz", 1)), 1)
            extra = 0.5 * stencil_from(padded, change, damping)
        fresh = solve(state + source + extra, state, damping)
        if rounds == 0:
            state = jnp.where(upper, state, fresh)
        elif rounds == STEPS:
            state = jnp.where(upper, fresh, state)
        else:
            state = fresh
    return state[None]


def solution(mesh):
    in_specs = (P("gx", "yz", None), P("gx", "yz", None), P("gx", "yz", None))
    out_specs = P("level", "gx", "yz", None)
    return jax.shard_map(
        per_device, mesh=mesh, in_specs=in_specs, out_specs=out_specs, check_vma=False
    )
```

profile of v0, /device:TPU:0, one launch (start us, length us, event | category | flops | bytes accessed | tf_op | source)
XLA Modules:
  0.0 858.0 jit_solution(10552199963659555347)
XLA Ops:
  0.7 4.9 collective-permute-start.1
  8.2 3.1 collective-permute-done
  12.6 4.7 collective-permute-start.3
  19.4 4.3 collective-permute-start.5
  25.2 4.2 collective-permute-done.4
  30.7 4.9 collective-permute-start.7
  38.3 40.1 %all-reduce.49 = (f32[]{:T(128)}, f32[]{:T(128)}) all-reduce(f32[]{:T(128)} %get-tuple-element.28, f32[]{:T(128)} %get-tuple-element.27), channel_id=1, replica_groups=mesh['level'=2,'gx'=4,'yz'=4] {'gx','yz'}, use_global_device_ids=true, to_apply=%region_1.2 | all-reduce | flops 2 | bytes 16 | tf_op jit(solution)/shard_map/psum | solution.py:49
  79.8 2.0 collective-permute-start.9
  83.3 8.2 collective-permute-done.8
  92.8 4.5 collective-permute-start.11
  97.6 1.4 collective-permute-done.11
  99.0 1.9 multiply_reduce_fusion.16
  100.9 39.7 %all-reduce.48 = (f32[]{:T(128)}, f32[]{:T(128)}) all-reduce(f32[]{:T(128)} %get-tuple-element.26, f32[]{:T(128)} %get-tuple-element.25), channel_id=1, replica_groups=mesh['level'=2,'gx'=4,'yz'=4] {'gx','yz'}, use_global_device_ids=true, to_apply=%region_5.6 | all-reduce | flops 2 | bytes 16 | tf_op jit(solution)/shard_map/psum | solution.py:49
  149.0 5.5 collective-permute-done.12
  155.9 4.5 collective-permute-start.15
  163.2 39.7 %all-reduce.47 = (f32[]{:T(128)}, f32[]{:T(128)}) all-reduce(f32[]{:T(128)} %get-tuple-element.24, f32[]{:T(128)} %get-tuple-element.23), channel_id=1, replica_groups=mesh['level'=2,'gx'=4,'yz'=4] {'gx','yz'}, use_global_device_ids=true, to_apply=%region_9.10 | all-reduce | flops 2 | bytes 16 | tf_op jit(solution)/shard_map/psum | solution.py:49
  212.1 7.1 collective-permute-start.18
  221.8 4.5 collective-permute-start.24
  227.8 4.7 collective-permute-start.20
  234.9 5.4 collective-permute-start.26
  241.8 5.1 collective-permute-done.25
  248.2 4.9 collective-permute-start.28
  255.8 39.8 %all-reduce.46 = (f32[]{:T(128)}, f32[]{:T(128)}) all-reduce(f32[]{:T(128)} %get-tuple-element.22, f32[]{:T(128)} %get-tuple-element.21), channel_id=1, replica_groups=mesh['level'=2,'gx'=4,'yz'=4] {'gx','yz'}, use_global_device_ids=true, to_apply=%region_13.14 | all-reduce | flops 2 | bytes 16 | tf_op jit(solution)/shard_map/psum | solution.py:49
  299.6 8.9 %collective-permute-done.29 = f32[1,16,256]{2,1,0:T(8,128)S(1)} collective-permute-done((f32[1,16,256]{2,1,0:T(8,128)S(1)}, f32[1,16,256]{2,1,0:T(8,128)S(1)}, u32[]{:S(2)}, u32[]{:S(2)}) %collective-permute-start.29) | collective-permute-done | bytes 16416 | tf_op jit(solution)/shard_map/ppermute | solution.py:21
  309.9 4.5 collective-permute-start.32
  316.0 1.9 multiply_reduce_fusion.11
  317.9 39.7 %all-reduce.45 = (f32[]{:T(128)}, f32[]{:T(128)}) all-reduce(f32[]{:T(128)} %get-tuple-element.20, f32[]{:T(128)} %get-tuple-element.19), channel_id=1, replica_groups=mesh['level'=2,'gx'=4,'yz'=4] {'gx','yz'}, use_global_device_ids=true, to_apply=%region_17.18 | all-reduce | flops 2 | bytes 16 | tf_op jit(solution)/shard_map/psum | solution.py:49
  366.0 5.5 collective-permute-done.33
  372.8 4.5 collective-permute-start.36
  377.6 1.4 collective-permute-done.36
  380.0 39.7 %all-reduce.44 = (f32[]{:T(128)}, f32[]{:T(128)}) all-reduce(f32[]{:T(128)} %get-tuple-element.18, f32[]{:T(128)} %get-tuple-element.17), channel_id=1, replica_groups=mesh['level'=2,'gx'=4,'yz'=4] {'gx','yz'}, use_global_device_ids=true, to_apply=%region_21.22 | all-reduce | flops 2 | bytes 16 | tf_op jit(solution)/shard_map/psum | solution.py:49
  426.3 1.4 collective-permute-start.42
  428.8 7.2 collective-permute-start.39
  438.6 4.5 collective-permute-start.45
  444.6 4.9 collective-permute-start.41
  451.7 5.4 collective-permute-start.47
  458.5 5.1 collective-permute-done.46
  465.0 4.9 collective-permute-start.49
  470.1 1.4 collective-permute-done.49
  472.6 39.8 %all-reduce.43 = (f32[]{:T(128)}, f32[]{:T(128)}) all-reduce(f32[]{:T(128)} %get-tuple-element.16, f32[]{:T(128)} %get-tuple-element.15), channel_id=1, replica_groups=mesh['level'=2,'gx'=4,'yz'=4] {'gx','yz'}, use_global_device_ids=true, to_apply=%region_25.26 | all-reduce | flops 2 | bytes 16 | tf_op jit(solution)/shard_map/psum | solution.py:49
  516.4 8.9 %collective-permute-done.50 = f32[1,16,256]{2,1,0:T(8,128)S(1)} collective-permute-done((f32[1,16,256]{2,1,0:T(8,128)S(1)}, f32[1,16,256]{2,1,0:T(8,128)S(1)}, u32[]{:S(2)}, u32[]{:S(2)}) %collective-permute-start.50) | collective-permute-done | bytes 16416 | tf_op jit(solution)/shard_map/ppermute | solution.py:21
  526.7 4.5 collective-permute-start.53
  531.4 1.4 collective-permute-done.53
  532.8 1.9 multiply_reduce_fusion.6
  534.7 39.8 %all-reduce.42 = (f32[]{:T(128)}, f32[]{:T(128)}) all-reduce(f32[]{:T(128)} %get-tuple-element.14, f32[]{:T(128)} %get-tuple-element.13), channel_id=1, replica_groups=mesh['level'=2,'gx'=4,'yz'=4] {'gx','yz'}, use_global_device_ids=true, to_apply=%region_29.30 | all-reduce | flops 2 | bytes 16 | tf_op jit(solution)/shard_map/psum | solution.py:49
  582.8 5.4 collective-permute-done.54
  589.6 4.5 collective-permute-start.57
  596.9 39.7 %all-reduce.41 = (f32[]{:T(128)}, f32[]{:T(128)}) all-reduce(f32[]{:T(128)} %get-tuple-element.12, f32[]{:T(128)} %get-tuple-element.11), channel_id=1, replica_groups=mesh['level'=2,'gx'=4,'yz'=4] {'gx','yz'}, use_global_device_ids=true, to_apply=%region_33.34 | all-reduce | flops 2 | bytes 16 | tf_op jit(solution)/shard_map/psum | solution.py:49
  643.1 1.4 collective-permute-start.63
  644.9 7.2 collective-permute-start.60
  654.7 4.5 collective-permute-start.66
  660.7 4.7 collective-permute-start.62
  667.8 5.4 collective-permute-start.68
  674.7 5.1 collective-permute-done.67
  681.1 4.9 collective-permute-start.70
  688.6 39.8 %all-reduce.40 = (f32[]{:T(128)}, f32[]{:T(128)}) all-reduce(f32[]{:T(128)} %get-tuple-element.10, f32[]{:T(128)} %get-tuple-element.9), channel_id=1, replica_groups=mesh['level'=2,'gx'=4,'yz'=4] {'gx','yz'}, use_global_device_ids=true, to_apply=%region_37.38 | all-reduce | flops 2 | bytes 16 | tf_op jit(solution)/shard_map/psum | solution.py:49
  732.7 8.9 %collective-permute-done.71 = f32[1,16,256]{2,1,0:T(8,128)S(1)} collective-permute-done((f32[1,16,256]{2,1,0:T(8,128)S(1)}, f32[1,16,256]{2,1,0:T(8,128)S(1)}, u32[]{:S(2)}, u32[]{:S(2)}) %collective-permute-start.71) | collective-permute-done | bytes 16416 | tf_op jit(solution)/shard_map/ppermute | solution.py:21
  743.0 4.5 collective-permute-start.74
  747.8 1.4 collective-permute-done.74
  749.1 1.9 multiply_reduce_fusion.1
  751.0 39.7 %all-reduce.39 = (f32[]{:T(128)}, f32[]{:T(128)}) all-reduce(f32[]{:T(128)} %get-tuple-element.8, f32[]{:T(128)} %get-tuple-element.7), channel_id=1, replica_groups=mesh['level'=2,'gx'=4,'yz'=4] {'gx','yz'}, use_global_device_ids=true, to_apply=%region_41.42 | all-reduce | flops 2 | bytes 16 | tf_op jit(solution)/shard_map/psum | solution.py:49
  799.2 5.5 collective-permute-done.75
  806.0 4.5 collective-permute-start.78
  813.3 39.7 %all-reduce.38 = (f32[]{:T(128)}, f32[]{:T(128)}) all-reduce(f32[]{:T(128)} %get-tuple-element.6, f32[]{:T(128)} %get-tuple-element.5), channel_id=1, replica_groups=mesh['level'=2,'gx'=4,'yz'=4] {'gx','yz'}, use_global_device_ids=true, to_apply=%region_45.46 | all-reduce | flops 2 | bytes 16 | tf_op jit(solution)/shard_map/psum | solution.py:49
  (217 shorter events, 107.2 us)
Async XLA Ops:
  0.7 6.3 collective-permute-start.1
  11.3 6.2 collective-permute-start.2
  12.6 6.3 collective-permute-start.3
  29.4 6.4 collective-permute-start.6
  30.7 6.5 collective-permute-start.7
  81.9 9.6 %collective-permute-start.8 = (f32[1,16,256]{2,1,0:T(8,128)S(1)}, f32[1,16,256]{2,1,0:T(8,128)S(1)}, u32[]{:S(2)}, u32[]{:S(2)}) collective-permute-start(f32[1,16,256]{2,1,0:T(8,128)S(1)} %get-tuple-element.164), channel_id=1, source_target_pairs={{4,0},{8,4},{12,8},{5,1},{9,5},{13,9},{6,2},{10,6},{14,10},{7,3},{... | collective-permute-start | bytes 49160 | tf_op jit(solution)/shard_map/ppermute | solution.py:21
  91.5 6.1 collective-permute-start.10
  92.8 6.2 collective-permute-start.11
  147.6 7.0 collective-permute-start.12
  154.6 6.1 collective-permute-start.14
  155.9 6.2 collective-permute-start.15
  208.4 12.0 %collective-permute-start.22 = (f32[1,16,256]{2,1,0:T(8,128)S(1)}, f32[1,16,256]{2,1,0:T(8,128)S(1)}, u32[]{:S(2)}, u32[]{:S(2)}) collective-permute-start(f32[1,16,256]{2,1,0:T(8,128)S(1)} %get-tuple-element.157), channel_id=1, source_target_pairs={{0,4},{4,8},{8,12},{1,5},{5,9},{9,13},{2,6},{6,10},{10,14},{3,7},{... | collective-permute-start | bytes 49160 | tf_op jit(solution)/shard_map/ppermute | solution.py:19
  209.7 10.7 %collective-permute-start.21 = (f32[1,16,256]{2,1,0:T(8,128)S(1)}, f32[1,16,256]{2,1,0:T(8,128)S(1)}, u32[]{:S(2)}, u32[]{:S(2)}) collective-permute-start(f32[1,16,256]{2,1,0:T(8,128)S(1)} %get-tuple-element.158), channel_id=1, source_target_pairs={{4,0},{8,4},{12,8},{5,1},{9,5},{13,9},{6,2},{10,6},{14,10},{7,3},{... | collective-permute-start | bytes 49160 | tf_op jit(solution)/shard_map/ppermute | solution.py:21
  212.1 14.3 %collective-permute-start.18 = (f32[1,16,256]{2,1,0:T(8,128)S(1)}, f32[1,16,256]{2,1,0:T(8,128)S(1)}, u32[]{:S(2)}, u32[]{:S(2)}) collective-permute-start(f32[1,16,256]{2,1,0:T(8,128)S(1)} %get-tuple-element.155), channel_id=1, source_target_pairs={{0,4},{4,8},{8,12},{1,5},{5,9},{9,13},{2,6},{6,10},{10,14},{3,7},{... | collective-permute-start | bytes 49160 | tf_op jit(solution)/shard_map/ppermute | solution.py:19
  219.2 7.2 collective-permute-start.17
  220.5 12.2 %collective-permute-start.23 = (f32[34,1,256]{2,1,0:T(1,128)S(1)}, f32[34,1,256]{2,1,0:T(1,128)S(1)}, u32[]{:S(2)}, u32[]{:S(2)}) collective-permute-start(f32[34,1,256]{2,1,0:T(1,128)S(1)} %get-tuple-element.89), channel_id=1, source_target_pairs={{1,0},{2,1},{3,2},{5,4},{6,5},{7,6},{9,8},{10,9},{11,10},{13,12},{... | collective-permute-start | bytes 104456 | tf_op jit(solution)/shard_map/ppermute | solution.py:21
  221.8 10.9 %collective-permute-start.24 = (f32[34,1,256]{2,1,0:T(1,128)S(1)}, f32[34,1,256]{2,1,0:T(1,128)S(1)}, u32[]{:S(2)}, u32[]{:S(2)}) collective-permute-start(f32[34,1,256]{2,1,0:T(1,128)S(1)} %get-tuple-element.90), channel_id=1, source_target_pairs={{0,1},{1,2},{2,3},{4,5},{5,6},{6,7},{8,9},{9,10},{10,11},{12,13},{... | collective-permute-start | bytes 104456 | tf_op jit(solution)/shard_map/ppermute | solution.py:19
  226.5 6.2 collective-permute-start.19
  227.8 6.3 collective-permute-start.20
  234.9 6.9 collective-permute-start.26
  240.3 6.5 collective-permute-start.25
  246.9 6.4 collective-permute-start.27
  248.2 6.5 collective-permute-start.28
  298.2 10.3 %collective-permute-start.29 = (f32[1,16,256]{2,1,0:T(8,128)S(1)}, f32[1,16,256]{2,1,0:T(8,128)S(1)}, u32[]{:S(2)}, u32[]{:S(2)}) collective-permute-start(f32[1,16,256]{2,1,0:T(8,128)S(1)} %get-tuple-element.144), channel_id=1, source_target_pairs={{4,0},{8,4},{12,8},{5,1},{9,5},{13,9},{6,2},{10,6},{14,10},{7,3},{... | collective-permute-start | bytes 49160 | tf_op jit(solution)/shard_map/ppermute | solution.py:21
  308.6 6.1 collective-permute-start.31
  309.9 6.2 collective-permute-start.32
  364.5 6.9 collective-permute-start.33
  371.5 6.1 collective-permute-start.35
  372.8 6.2 collective-permute-start.36
  425.0 12.3 %collective-permute-start.43 = (f32[1,16,256]{2,1,0:T(8,128)S(1)}, f32[1,16,256]{2,1,0:T(8,128)S(1)}, u32[]{:S(2)}, u32[]{:S(2)}) collective-permute-start(f32[1,16,256]{2,1,0:T(8,128)S(1)} %get-tuple-element.137), channel_id=1, source_target_pairs={{0,4},{4,8},{8,12},{1,5},{5,9},{9,13},{2,6},{6,10},{10,14},{3,7},{... | collective-permute-start | bytes 49160 | tf_op jit(solution)/shard_map/ppermute | solution.py:19
  426.3 11.0 %collective-permute-start.42 = (f32[1,16,256]{2,1,0:T(8,128)S(1)}, f32[1,16,256]{2,1,0:T(8,128)S(1)}, u32[]{:S(2)}, u32[]{:S(2)}) collective-permute-start(f32[1,16,256]{2,1,0:T(8,128)S(1)} %get-tuple-element.138), channel_id=1, source_target_pairs={{4,0},{8,4},{12,8},{5,1},{9,5},{13,9},{6,2},{10,6},{14,10},{7,3},{... | collective-permute-start | bytes 49160 | tf_op jit(solution)/shard_map/ppermute | solution.py:21
  428.8 14.4 %collective-permute-start.39 = (f32[1,16,256]{2,1,0:T(8,128)S(1)}, f32[1,16,256]{2,1,0:T(8,128)S(1)}, u32[]{:S(2)}, u32[]{:S(2)}) collective-permute-start(f32[1,16,256]{2,1,0:T(8,128)S(1)} %get-tuple-element.135), channel_id=1, source_target_pairs={{0,4},{4,8},{8,12},{1,5},{5,9},{9,13},{2,6},{6,10},{10,14},{3,7},{... | collective-permute-start | bytes 49160 | tf_op jit(solution)/shard_map/ppermute | solution.py:19
  435.9 7.2 collective-permute-start.38
  437.3 12.3 %collective-permute-start.44 = (f32[34,1,256]{2,1,0:T(1,128)S(1)}, f32[34,1,256]{2,1,0:T(1,128)S(1)}, u32[]{:S(2)}, u32[]{:S(2)}) collective-permute-start(f32[34,1,256]{2,1,0:T(1,128)S(1)} %get-tuple-element.79), channel_id=1, source_target_pairs={{1,0},{2,1},{3,2},{5,4},{6,5},{7,6},{9,8},{10,9},{11,10},{13,12},{... | collective-permute-start | bytes 104456 | tf_op jit(solution)/shard_map/ppermute | solution.py:21
  438.6 11.0 %collective-permute-start.45 = (f32[34,1,256]{2,1,0:T(1,128)S(1)}, f32[34,1,256]{2,1,0:T(1,128)S(1)}, u32[]{:S(2)}, u32[]{:S(2)}) collective-permute-start(f32[34,1,256]{2,1,0:T(1,128)S(1)} %get-tuple-element.80), channel_id=1, source_target_pairs={{0,1},{1,2},{2,3},{4,5},{5,6},{6,7},{8,9},{9,10},{10,11},{12,13},{... | collective-permute-start | bytes 104456 | tf_op jit(solution)/shard_map/ppermute | solution.py:19
  443.3 6.4 collective-permute-start.40
  444.6 6.3 collective-permute-start.41
  451.7 6.9 collective-permute-start.47
  457.1 6.5 collective-permute-start.46
  463.7 6.4 collective-permute-start.48
  465.0 6.5 collective-permute-start.49
  515.0 10.4 %collective-permute-start.50 = (f32[1,16,256]{2,1,0:T(8,128)S(1)}, f32[1,16,256]{2,1,0:T(8,128)S(1)}, u32[]{:S(2)}, u32[]{:S(2)}) collective-permute-start(f32[1,16,256]{2,1,0:T(8,128)S(1)} %get-tuple-element.124), channel_id=1, source_target_pairs={{4,0},{8,4},{12,8},{5,1},{9,5},{13,9},{6,2},{10,6},{14,10},{7,3},{... | collective-permute-start | bytes 49160 | tf_op jit(solution)/shard_map/ppermute | solution.py:21
  526.7 6.2 collective-permute-start.53
  581.4 6.9 collective-permute-start.54
  588.3 6.1 collective-permute-start.56
  589.6 6.2 collective-permute-start.57
  641.8 11.6 %collective-permute-start.64 = (f32[1,16,256]{2,1,0:T(8,128)S(1)}, f32[1,16,256]{2,1,0:T(8,128)S(1)}, u32[]{:S(2)}, u32[]{:S(2)}) collective-permute-start(f32[1,16,256]{2,1,0:T(8,128)S(1)} %get-tuple-element.117), channel_id=1, source_target_pairs={{0,4},{4,8},{8,12},{1,5},{5,9},{9,13},{2,6},{6,10},{10,14},{3,7},{... | collective-permute-start | bytes 49160 | tf_op jit(solution)/shard_map/ppermute | solution.py:19
  643.1 10.3 %collective-permute-start.63 = (f32[1,16,256]{2,1,0:T(8,128)S(1)}, f32[1,16,256]{2,1,0:T(8,128)S(1)}, u32[]{:S(2)}, u32[]{:S(2)}) collective-permute-start(f32[1,16,256]{2,1,0:T(8,128)S(1)} %get-tuple-element.118), channel_id=1, source_target_pairs={{4,0},{8,4},{12,8},{5,1},{9,5},{13,9},{6,2},{10,6},{14,10},{7,3},{... | collective-permute-start | bytes 49160 | tf_op jit(solution)/shard_map/ppermute | solution.py:21
  644.9 14.4 %collective-permute-start.60 = (f32[1,16,256]{2,1,0:T(8,128)S(1)}, f32[1,16,256]{2,1,0:T(8,128)S(1)}, u32[]{:S(2)}, u32[]{:S(2)}) collective-permute-start(f32[1,16,256]{2,1,0:T(8,128)S(1)} %get-tuple-element.115), channel_id=1, source_target_pairs={{0,4},{4,8},{8,12},{1,5},{5,9},{9,13},{2,6},{6,10},{10,14},{3,7},{... | collective-permute-start | bytes 49160 | tf_op jit(solution)/shard_map/ppermute | solution.py:19
  652.1 7.2 collective-permute-start.59
  653.4 12.2 %collective-permute-start.65 = (f32[34,1,256]{2,1,0:T(1,128)S(1)}, f32[34,1,256]{2,1,0:T(1,128)S(1)}, u32[]{:S(2)}, u32[]{:S(2)}) collective-permute-start(f32[34,1,256]{2,1,0:T(1,128)S(1)} %get-tuple-element.69), channel_id=1, source_target_pairs={{1,0},{2,1},{3,2},{5,4},{6,5},{7,6},{9,8},{10,9},{11,10},{13,12},{... | collective-permute-start | bytes 104456 | tf_op jit(solution)/shard_map/ppermute | solution.py:21
  654.7 10.9 %collective-permute-start.66 = (f32[34,1,256]{2,1,0:T(1,128)S(1)}, f32[34,1,256]{2,1,0:T(1,128)S(1)}, u32[]{:S(2)}, u32[]{:S(2)}) collective-permute-start(f32[34,1,256]{2,1,0:T(1,128)S(1)} %get-tuple-element.70), channel_id=1, source_target_pairs={{0,1},{1,2},{2,3},{4,5},{5,6},{6,7},{8,9},{9,10},{10,11},{12,13},{... | collective-permute-start | bytes 104456 | tf_op jit(solution)/shard_map/ppermute | solution.py:19
  659.4 6.2 collective-permute-start.61
  660.7 6.3 collective-permute-start.62
  667.8 6.9 collective-permute-start.68
  673.2 6.5 collective-permute-start.67
  679.8 6.4 collective-permute-start.69
  681.1 6.5 collective-permute-start.70
  731.3 10.4 %collective-permute-start.71 = (f32[1,16,256]{2,1,0:T(8,128)S(1)}, f32[1,16,256]{2,1,0:T(8,128)S(1)}, u32[]{:S(2)}, u32[]{:S(2)}) collective-permute-start(f32[1,16,256]{2,1,0:T(8,128)S(1)} %get-tuple-element.104), channel_id=1, source_target_pairs={{4,0},{8,4},{12,8},{5,1},{9,5},{13,9},{6,2},{10,6},{14,10},{7,3},{... | collective-permute-start | bytes 49160 | tf_op jit(solution)/shard_map/ppermute | solution.py:21
  741.7 6.1 collective-permute-start.73
  743.0 6.2 collective-permute-start.74
  797.7 6.9 collective-permute-start.75
  804.7 6.1 collective-permute-start.77
  806.0 6.2 collective-permute-start.78
  (25 other events, 105.0 us)
where the time goes:
time: 861 us; the launch traced here: 858 us
  blocking collectives  477 us (55%)
  starting transfers between devices  204 us (24%)
  waiting for transfers between devices  103 us (12%)
  between operations  39.6 us (5%)
  other arithmetic  27.4 us (3%)
    psum x12, blocking collectives, two_products(): lax.psum((jnp.sum(resid * resid), jnp.sum(resid * image)), ('gx', 'yz'))  477 us
    ppermute x38, starting transfers between devices, extended(): lax.ppermute(tail, axis, [(i, (i + 1) % count) for i in range(ends)])  150 us
    ppermute x38, waiting for transfers between devices, extended(): lax.ppermute(head, axis, [((i + 1) % count, i) for i in range(ends)])  79.6 us
    ppermute x38, starting transfers between devices, extended(): lax.ppermute(head, axis, [((i + 1) % count, i) for i in range(ends)])  49.4 us
    ppermute x38, waiting for transfers between devices, extended(): lax.ppermute(tail, axis, [(i, (i + 1) % count) for i in range(ends)])  23.4 us
  transfers between devices with their start and end apart: 79, of which 42 were waited for; matrix products, arithmetic and copies ran while one was open for 1% of the time, Pallas kernels for 0%

commit v1 on v0

--- a/solution.py
+++ b/solution.py
@@ -46,7 +46,7 @@
 
 
 def two_products(resid, image):
-    return lax.psum((jnp.sum(resid * resid), jnp.sum(resid * image)), ("gx", "yz"))
+    return lax.psum(lax.psum((jnp.sum(resid * resid), jnp.sum(resid * image)), "gx"), "yz")
 
 
 def solve(target, guess, damping):

time: 861 us -> 641 us (0.74)
  blocking collectives: 477 us -> 272 us
  waiting for transfers between devices: 103 us -> 88.5 us
    psum x12 -> x24, blocking collectives: 477 us -> 272 us  [the longest x12 141 us: two_products(): lax.psum(lax.psum((jnp.sum(resid * resid), jnp.sum(resid * image)), 'gx')...]
    ppermute x38, waiting for transfers between devices: 79.6 us -> 64.9 us  [extended(): lax.ppermute(head, axis, [((i + 1) % count, i) for i in range(ends)])]
where the time goes in v1:
time: 641 us; the launch traced here: 637 us
  blocking collectives  272 us (42%)
  starting transfers between devices  203 us (32%)
  waiting for transfers between devices  88.5 us (14%)
  between operations  39.3 us (6%)
  other arithmetic  27.1 us (4%)
  local copies, waits for them, and re-layouts  7.39 us (1%)
    ppermute x38, starting transfers between devices, extended(): lax.ppermute(tail, axis, [(i, (i + 1) % count) for i in range(ends)])  150 us
    psum x12, blocking collectives, two_products(): lax.psum(lax.psum((jnp.sum(resid * resid), jnp.sum(resid * image)), 'gx')...  141 us
    psum x12, blocking collectives, two_products(): lax.psum((jnp.sum(resid * resid), jnp.sum(resid * image)), 'gx')  131 us
    ppermute x38, waiting for transfers between devices, extended(): lax.ppermute(head, axis, [((i + 1) % count, i) for i in range(ends)])  64.9 us
    ppermute x38, starting transfers between devices, extended(): lax.ppermute(head, axis, [((i + 1) % count, i) for i in range(ends)])  49.5 us
    ppermute x38, waiting for transfers between devices, extended(): lax.ppermute(tail, axis, [(i, (i + 1) % count) for i in range(ends)])  23.6 us
    reduce_sum x12, other arithmetic, two_products(): jnp.sum(resid * image)  16 us
  transfers between devices with their start and end apart: 79, of which 42 were waited for; matrix products, arithmetic and copies ran while one was open for 1% of the time, Pallas kernels for 0%

profile of v1, /device:TPU:0, one launch (start us, length us, event | category | flops | bytes accessed | tf_op | source)
XLA Modules:
  0.0 637.2 jit_solution(12951947392990534814)
XLA Ops:
  0.7 4.9 collective-permute-start.1
  8.2 3.1 collective-permute-done
  12.6 4.7 collective-permute-start.3
  19.4 4.3 collective-permute-start.5
  25.2 4.2 collective-permute-done.4
  30.7 4.9 collective-permute-start.7
  38.2 9.6 %all-reduce.61 = (f32[]{:T(128)}, f32[]{:T(128)}) all-reduce(f32[]{:T(128)} %get-tuple-element.28, f32[]{:T(128)} %get-tuple-element.27), channel_id=1, replica_groups=mesh['level'=2,'gx'=4,'yz'=4] {'gx'}, use_global_device_ids=true, to_apply=%region_1.2 | all-reduce | flops 2 | bytes 16 | tf_op jit(solution)/shard_map/psum | solution.py:49
  47.9 13.8 %all-reduce.49 = (f32[]{:T(128)}, f32[]{:T(128)}) all-reduce(f32[]{:T(128)} %get-tuple-element.75, f32[]{:T(128)} %get-tuple-element.76), channel_id=1, replica_groups=mesh['level'=2,'gx'=4,'yz'=4] {'yz'}, use_global_device_ids=true, to_apply=%region_2.3 | all-reduce | flops 2 | bytes 16 | tf_op jit(solution)/shard_map/psum | solution.py:49
  66.8 4.6 collective-permute-done.8
  72.8 4.5 collective-permute-start.11
  80.8 11.0 %all-reduce.60 = (f32[]{:T(128)}, f32[]{:T(128)}) all-reduce(f32[]{:T(128)} %get-tuple-element.26, f32[]{:T(128)} %get-tuple-element.25), channel_id=1, replica_groups=mesh['level'=2,'gx'=4,'yz'=4] {'gx'}, use_global_device_ids=true, to_apply=%region_7.8 | all-reduce | flops 2 | bytes 16 | tf_op jit(solution)/shard_map/psum | solution.py:49
  91.8 11.3 %all-reduce.48 = (f32[]{:T(128)}, f32[]{:T(128)}) all-reduce(f32[]{:T(128)} %get-tuple-element.73, f32[]{:T(128)} %get-tuple-element.74), channel_id=1, replica_groups=mesh['level'=2,'gx'=4,'yz'=4] {'yz'}, use_global_device_ids=true, to_apply=%region_8.9 | all-reduce | flops 2 | bytes 16 | tf_op jit(solution)/shard_map/psum | solution.py:49
  111.8 5.4 collective-permute-done.12
  118.5 4.5 collective-permute-start.15
  125.8 11.0 %all-reduce.59 = (f32[]{:T(128)}, f32[]{:T(128)}) all-reduce(f32[]{:T(128)} %get-tuple-element.24, f32[]{:T(128)} %get-tuple-element.23), channel_id=1, replica_groups=mesh['level'=2,'gx'=4,'yz'=4] {'gx'}, use_global_device_ids=true, to_apply=%region_13.14 | all-reduce | flops 2 | bytes 16 | tf_op jit(solution)/shard_map/psum | solution.py:49
  136.7 11.3 %all-reduce.47 = (f32[]{:T(128)}, f32[]{:T(128)}) all-reduce(f32[]{:T(128)} %get-tuple-element.71, f32[]{:T(128)} %get-tuple-element.72), channel_id=1, replica_groups=mesh['level'=2,'gx'=4,'yz'=4] {'yz'}, use_global_device_ids=true, to_apply=%region_14.15 | all-reduce | flops 2 | bytes 16 | tf_op jit(solution)/shard_map/psum | solution.py:49
  157.5 5.7 collective-permute-start.18
  165.9 4.5 collective-permute-start.24
  171.8 4.7 collective-permute-start.20
  178.9 5.4 collective-permute-start.26
  185.8 5.1 collective-permute-done.25
  192.2 4.9 collective-permute-start.28
  199.8 11.0 %all-reduce.58 = (f32[]{:T(128)}, f32[]{:T(128)}) all-reduce(f32[]{:T(128)} %get-tuple-element.22, f32[]{:T(128)} %get-tuple-element.21), channel_id=1, replica_groups=mesh['level'=2,'gx'=4,'yz'=4] {'gx'}, use_global_device_ids=true, to_apply=%region_19.20 | all-reduce | flops 2 | bytes 16 | tf_op jit(solution)/shard_map/psum | solution.py:49
  210.8 12.3 %all-reduce.46 = (f32[]{:T(128)}, f32[]{:T(128)}) all-reduce(f32[]{:T(128)} %get-tuple-element.69, f32[]{:T(128)} %get-tuple-element.70), channel_id=1, replica_groups=mesh['level'=2,'gx'=4,'yz'=4] {'yz'}, use_global_device_ids=true, to_apply=%region_20.21 | all-reduce | flops 2 | bytes 16 | tf_op jit(solution)/shard_map/psum | solution.py:49
  227.5 5.4 collective-permute-done.29
  234.2 4.5 collective-permute-start.32
  242.3 11.0 %all-reduce.57 = (f32[]{:T(128)}, f32[]{:T(128)}) all-reduce(f32[]{:T(128)} %get-tuple-element.20, f32[]{:T(128)} %get-tuple-element.19), channel_id=1, replica_groups=mesh['level'=2,'gx'=4,'yz'=4] {'gx'}, use_global_device_ids=true, to_apply=%region_25.26 | all-reduce | flops 2 | bytes 16 | tf_op jit(solution)/shard_map/psum | solution.py:49
  253.3 11.3 %all-reduce.45 = (f32[]{:T(128)}, f32[]{:T(128)}) all-reduce(f32[]{:T(128)} %get-tuple-element.67, f32[]{:T(128)} %get-tuple-element.68), channel_id=1, replica_groups=mesh['level'=2,'gx'=4,'yz'=4] {'yz'}, use_global_device_ids=true, to_apply=%region_26.27 | all-reduce | flops 2 | bytes 16 | tf_op jit(solution)/shard_map/psum | solution.py:49
  273.3 5.4 collective-permute-done.33
  280.0 4.5 collective-permute-start.36
  287.3 11.0 %all-reduce.56 = (f32[]{:T(128)}, f32[]{:T(128)}) all-reduce(f32[]{:T(128)} %get-tuple-element.18, f32[]{:T(128)} %get-tuple-element.17), channel_id=1, replica_groups=mesh['level'=2,'gx'=4,'yz'=4] {'gx'}, use_global_device_ids=true, to_apply=%region_31.32 | all-reduce | flops 2 | bytes 16 | tf_op jit(solution)/shard_map/psum | solution.py:49
  298.3 11.3 %all-reduce.44 = (f32[]{:T(128)}, f32[]{:T(128)}) all-reduce(f32[]{:T(128)} %get-tuple-element.65, f32[]{:T(128)} %get-tuple-element.66), channel_id=1, replica_groups=mesh['level'=2,'gx'=4,'yz'=4] {'yz'}, use_global_device_ids=true, to_apply=%region_32.33 | all-reduce | flops 2 | bytes 16 | tf_op jit(solution)/shard_map/psum | solution.py:49
  319.2 5.7 collective-permute-start.39
  327.8 4.5 collective-permute-start.45
  333.7 4.7 collective-permute-start.41
  340.8 5.4 collective-permute-start.47
  347.7 5.1 collective-permute-done.46
  354.1 4.9 collective-permute-start.49
  361.7 11.0 %all-reduce.55 = (f32[]{:T(128)}, f32[]{:T(128)}) all-reduce(f32[]{:T(128)} %get-tuple-element.16, f32[]{:T(128)} %get-tuple-element.15), channel_id=1, replica_groups=mesh['level'=2,'gx'=4,'yz'=4] {'gx'}, use_global_device_ids=true, to_apply=%region_37.38 | all-reduce | flops 2 | bytes 16 | tf_op jit(solution)/shard_map/psum | solution.py:49
  372.7 12.2 %all-reduce.43 = (f32[]{:T(128)}, f32[]{:T(128)}) all-reduce(f32[]{:T(128)} %get-tuple-element.63, f32[]{:T(128)} %get-tuple-element.64), channel_id=1, replica_groups=mesh['level'=2,'gx'=4,'yz'=4] {'yz'}, use_global_device_ids=true, to_apply=%region_38.39 | all-reduce | flops 2 | bytes 16 | tf_op jit(solution)/shard_map/psum | solution.py:49
  389.4 5.4 collective-permute-done.50
  396.1 4.5 collective-permute-start.53
  404.2 11.0 %all-reduce.54 = (f32[]{:T(128)}, f32[]{:T(128)}) all-reduce(f32[]{:T(128)} %get-tuple-element.14, f32[]{:T(128)} %get-tuple-element.13), channel_id=1, replica_groups=mesh['level'=2,'gx'=4,'yz'=4] {'gx'}, use_global_device_ids=true, to_apply=%region_43.44 | all-reduce | flops 2 | bytes 16 | tf_op jit(solution)/shard_map/psum | solution.py:49
  415.2 11.3 %all-reduce.42 = (f32[]{:T(128)}, f32[]{:T(128)}) all-reduce(f32[]{:T(128)} %get-tuple-element.61, f32[]{:T(128)} %get-tuple-element.62), channel_id=1, replica_groups=mesh['level'=2,'gx'=4,'yz'=4] {'yz'}, use_global_device_ids=true, to_apply=%region_44.45 | all-reduce | flops 2 | bytes 16 | tf_op jit(solution)/shard_map/psum | solution.py:49
  435.2 5.4 collective-permute-done.54
  441.9 4.5 collective-permute-start.57
  449.2 11.0 %all-reduce.53 = (f32[]{:T(128)}, f32[]{:T(128)}) all-reduce(f32[]{:T(128)} %get-tuple-element.12, f32[]{:T(128)} %get-tuple-element.11), channel_id=1, replica_groups=mesh['level'=2,'gx'=4,'yz'=4] {'gx'}, use_global_device_ids=true, to_apply=%region_49.50 | all-reduce | flops 2 | bytes 16 | tf_op jit(solution)/shard_map/psum | solution.py:49
  460.2 11.3 %all-reduce.41 = (f32[]{:T(128)}, f32[]{:T(128)}) all-reduce(f32[]{:T(128)} %get-tuple-element.59, f32[]{:T(128)} %get-tuple-element.60), channel_id=1, replica_groups=mesh['level'=2,'gx'=4,'yz'=4] {'yz'}, use_global_device_ids=true, to_apply=%region_50.51 | all-reduce | flops 2 | bytes 16 | tf_op jit(solution)/shard_map/psum | solution.py:49
  480.4 5.7 collective-permute-start.60
  488.8 4.5 collective-permute-start.66
  494.7 4.7 collective-permute-start.62
  501.8 5.4 collective-permute-start.68
  508.7 5.1 collective-permute-done.67
  515.2 4.9 collective-permute-start.70
  522.7 11.0 %all-reduce.52 = (f32[]{:T(128)}, f32[]{:T(128)}) all-reduce(f32[]{:T(128)} %get-tuple-element.10, f32[]{:T(128)} %get-tuple-element.9), channel_id=1, replica_groups=mesh['level'=2,'gx'=4,'yz'=4] {'gx'}, use_global_device_ids=true, to_apply=%region_55.56 | all-reduce | flops 2 | bytes 16 | tf_op jit(solution)/shard_map/psum | solution.py:49
  533.7 12.2 %all-reduce.40 = (f32[]{:T(128)}, f32[]{:T(128)}) all-reduce(f32[]{:T(128)} %get-tuple-element.57, f32[]{:T(128)} %get-tuple-element.58), channel_id=1, replica_groups=mesh['level'=2,'gx'=4,'yz'=4] {'yz'}, use_global_device_ids=true, to_apply=%region_56.57 | all-reduce | flops 2 | bytes 16 | tf_op jit(solution)/shard_map/psum | solution.py:49
  550.3 5.4 collective-permute-done.71
  557.1 4.5 collective-permute-start.74
  565.1 11.0 %all-reduce.51 = (f32[]{:T(128)}, f32[]{:T(128)}) all-reduce(f32[]{:T(128)} %get-tuple-element.8, f32[]{:T(128)} %get-tuple-element.7), channel_id=1, replica_groups=mesh['level'=2,'gx'=4,'yz'=4] {'gx'}, use_global_device_ids=true, to_apply=%region_61.62 | all-reduce | flops 2 | bytes 16 | tf_op jit(solution)/shard_map/psum | solution.py:49
  576.1 11.3 %all-reduce.39 = (f32[]{:T(128)}, f32[]{:T(128)}) all-reduce(f32[]{:T(128)} %get-tuple-element.55, f32[]{:T(128)} %get-tuple-element.56), channel_id=1, replica_groups=mesh['level'=2,'gx'=4,'yz'=4] {'yz'}, use_global_device_ids=true, to_apply=%region_62.63 | all-reduce | flops 2 | bytes 16 | tf_op jit(solution)/shard_map/psum | solution.py:49
  596.1 5.4 collective-permute-done.75
  602.8 4.5 collective-permute-start.78
  610.0 11.0 %all-reduce.50 = (f32[]{:T(128)}, f32[]{:T(128)}) all-reduce(f32[]{:T(128)} %get-tuple-element.6, f32[]{:T(128)} %get-tuple-element.5), channel_id=1, replica_groups=mesh['level'=2,'gx'=4,'yz'=4] {'gx'}, use_global_device_ids=true, to_apply=%region_67.68 | all-reduce | flops 2 | bytes 16 | tf_op jit(solution)/shard_map/psum | solution.py:49
  621.0 11.3 %all-reduce.38 = (f32[]{:T(128)}, f32[]{:T(128)}) all-reduce(f32[]{:T(128)} %get-tuple-element.53, f32[]{:T(128)} %get-tuple-element.54), channel_id=1, replica_groups=mesh['level'=2,'gx'=4,'yz'=4] {'yz'}, use_global_device_ids=true, to_apply=%region_68.69 | all-reduce | flops 2 | bytes 16 | tf_op jit(solution)/shard_map/psum | solution.py:49
  (229 shorter events, 130.4 us)
Async XLA Ops:
  0.7 6.3 collective-permute-start.1
  11.3 6.2 collective-permute-start.2
  12.6 6.3 collective-permute-start.3
  29.4 6.4 %collective-permute-start.6 = (f32[34,1,256]{2,1,0:T(1,128)S(1)}, f32[34,1,256]{2,1,0:T(1,128)S(1)}, u32[]{:S(2)}, u32[]{:S(2)}) collective-permute-start(f32[34,1,256]{2,1,0:T(1,128)S(1)} %get-tuple-element.119), channel_id=1, source_target_pairs={{1,0},{2,1},{3,2},{5,4},{6,5},{7,6},{9,8},{10,9},{11,10},{13,12},{... | collective-permute-start | bytes 104456 | tf_op jit(solution)/shard_map/ppermute | solution.py:21
  30.7 6.5 %collective-permute-start.7 = (f32[34,1,256]{2,1,0:T(1,128)S(1)}, f32[34,1,256]{2,1,0:T(1,128)S(1)}, u32[]{:S(2)}, u32[]{:S(2)}) collective-permute-start(f32[34,1,256]{2,1,0:T(1,128)S(1)} %get-tuple-element.120), channel_id=1, source_target_pairs={{0,1},{1,2},{2,3},{4,5},{5,6},{6,7},{8,9},{9,10},{10,11},{12,13},{... | collective-permute-start | bytes 104456 | tf_op jit(solution)/shard_map/ppermute | solution.py:19
  71.5 6.1 collective-permute-start.10
  72.8 6.2 collective-permute-start.11
  110.4 6.8 %collective-permute-start.12 = (f32[1,16,256]{2,1,0:T(8,128)S(1)}, f32[1,16,256]{2,1,0:T(8,128)S(1)}, u32[]{:S(2)}, u32[]{:S(2)}) collective-permute-start(f32[1,16,256]{2,1,0:T(8,128)S(1)} %get-tuple-element.186), channel_id=1, source_target_pairs={{4,0},{8,4},{12,8},{5,1},{9,5},{13,9},{6,2},{10,6},{14,10},{7,3},{... | collective-permute-start | bytes 49160 | tf_op jit(solution)/shard_map/ppermute | solution.py:21
  117.2 6.1 collective-permute-start.14
  118.5 6.2 collective-permute-start.15
  153.5 11.0 %collective-permute-start.22 = (f32[1,16,256]{2,1,0:T(8,128)S(1)}, f32[1,16,256]{2,1,0:T(8,128)S(1)}, u32[]{:S(2)}, u32[]{:S(2)}) collective-permute-start(f32[1,16,256]{2,1,0:T(8,128)S(1)} %get-tuple-element.181), channel_id=1, source_target_pairs={{0,4},{4,8},{8,12},{1,5},{5,9},{9,13},{2,6},{6,10},{10,14},{3,7},{... | collective-permute-start | bytes 49160 | tf_op jit(solution)/shard_map/ppermute | solution.py:19
  155.1 9.3 %collective-permute-start.21 = (f32[1,16,256]{2,1,0:T(8,128)S(1)}, f32[1,16,256]{2,1,0:T(8,128)S(1)}, u32[]{:S(2)}, u32[]{:S(2)}) collective-permute-start(f32[1,16,256]{2,1,0:T(8,128)S(1)} %get-tuple-element.182), channel_id=1, source_target_pairs={{4,0},{8,4},{12,8},{5,1},{9,5},{13,9},{6,2},{10,6},{14,10},{7,3},{... | collective-permute-start | bytes 49160 | tf_op jit(solution)/shard_map/ppermute | solution.py:21
  157.5 12.9 %collective-permute-start.18 = (f32[1,16,256]{2,1,0:T(8,128)S(1)}, f32[1,16,256]{2,1,0:T(8,128)S(1)}, u32[]{:S(2)}, u32[]{:S(2)}) collective-permute-start(f32[1,16,256]{2,1,0:T(8,128)S(1)} %get-tuple-element.179), channel_id=1, source_target_pairs={{0,4},{4,8},{8,12},{1,5},{5,9},{9,13},{2,6},{6,10},{10,14},{3,7},{... | collective-permute-start | bytes 49160 | tf_op jit(solution)/shard_map/ppermute | solution.py:19
  163.2 7.2 %collective-permute-start.17 = (f32[1,16,256]{2,1,0:T(8,128)S(1)}, f32[1,16,256]{2,1,0:T(8,128)S(1)}, u32[]{:S(2)}, u32[]{:S(2)}) collective-permute-start(f32[1,16,256]{2,1,0:T(8,128)S(1)} %get-tuple-element.180), channel_id=1, source_target_pairs={{4,0},{8,4},{12,8},{5,1},{9,5},{13,9},{6,2},{10,6},{14,10},{7,3},{... | collective-permute-start | bytes 49160 | tf_op jit(solution)/shard_map/ppermute | solution.py:21
  164.6 12.2 %collective-permute-start.23 = (f32[34,1,256]{2,1,0:T(1,128)S(1)}, f32[34,1,256]{2,1,0:T(1,128)S(1)}, u32[]{:S(2)}, u32[]{:S(2)}) collective-permute-start(f32[34,1,256]{2,1,0:T(1,128)S(1)} %get-tuple-element.113), channel_id=1, source_target_pairs={{1,0},{2,1},{3,2},{5,4},{6,5},{7,6},{9,8},{10,9},{11,10},{13,12},{... | collective-permute-start | bytes 104456 | tf_op jit(solution)/shard_map/ppermute | solution.py:21
  165.9 10.9 %collective-permute-start.24 = (f32[34,1,256]{2,1,0:T(1,128)S(1)}, f32[34,1,256]{2,1,0:T(1,128)S(1)}, u32[]{:S(2)}, u32[]{:S(2)}) collective-permute-start(f32[34,1,256]{2,1,0:T(1,128)S(1)} %get-tuple-element.114), channel_id=1, source_target_pairs={{0,1},{1,2},{2,3},{4,5},{5,6},{6,7},{8,9},{9,10},{10,11},{12,13},{... | collective-permute-start | bytes 104456 | tf_op jit(solution)/shard_map/ppermute | solution.py:19
  170.5 6.2 collective-permute-start.19
  171.8 6.3 collective-permute-start.20
  178.9 6.9 %collective-permute-start.26 = (f32[1,16,256]{2,1,0:T(8,128)S(1)}, f32[1,16,256]{2,1,0:T(8,128)S(1)}, u32[]{:S(2)}, u32[]{:S(2)}) collective-permute-start(f32[1,16,256]{2,1,0:T(8,128)S(1)} %get-tuple-element.171), channel_id=1, source_target_pairs={{0,4},{4,8},{8,12},{1,5},{5,9},{9,13},{2,6},{6,10},{10,14},{3,7},{... | collective-permute-start | bytes 49160 | tf_op jit(solution)/shard_map/ppermute | solution.py:19
  184.4 6.5 %collective-permute-start.25 = (f32[1,16,256]{2,1,0:T(8,128)S(1)}, f32[1,16,256]{2,1,0:T(8,128)S(1)}, u32[]{:S(2)}, u32[]{:S(2)}) collective-permute-start(f32[1,16,256]{2,1,0:T(8,128)S(1)} %get-tuple-element.172), channel_id=1, source_target_pairs={{4,0},{8,4},{12,8},{5,1},{9,5},{13,9},{6,2},{10,6},{14,10},{7,3},{... | collective-permute-start | bytes 49160 | tf_op jit(solution)/shard_map/ppermute | solution.py:21
  190.9 6.4 %collective-permute-start.27 = (f32[34,1,256]{2,1,0:T(1,128)S(1)}, f32[34,1,256]{2,1,0:T(1,128)S(1)}, u32[]{:S(2)}, u32[]{:S(2)}) collective-permute-start(f32[34,1,256]{2,1,0:T(1,128)S(1)} %get-tuple-element.109), channel_id=1, source_target_pairs={{1,0},{2,1},{3,2},{5,4},{6,5},{7,6},{9,8},{10,9},{11,10},{13,12},{... | collective-permute-start | bytes 104456 | tf_op jit(solution)/shard_map/ppermute | solution.py:21
  192.2 6.5 %collective-permute-start.28 = (f32[34,1,256]{2,1,0:T(1,128)S(1)}, f32[34,1,256]{2,1,0:T(1,128)S(1)}, u32[]{:S(2)}, u32[]{:S(2)}) collective-permute-start(f32[34,1,256]{2,1,0:T(1,128)S(1)} %get-tuple-element.110), channel_id=1, source_target_pairs={{0,1},{1,2},{2,3},{4,5},{5,6},{6,7},{8,9},{9,10},{10,11},{12,13},{... | collective-permute-start | bytes 104456 | tf_op jit(solution)/shard_map/ppermute | solution.py:19
  226.1 6.8 %collective-permute-start.29 = (f32[1,16,256]{2,1,0:T(8,128)S(1)}, f32[1,16,256]{2,1,0:T(8,128)S(1)}, u32[]{:S(2)}, u32[]{:S(2)}) collective-permute-start(f32[1,16,256]{2,1,0:T(8,128)S(1)} %get-tuple-element.168), channel_id=1, source_target_pairs={{4,0},{8,4},{12,8},{5,1},{9,5},{13,9},{6,2},{10,6},{14,10},{7,3},{... | collective-permute-start | bytes 49160 | tf_op jit(solution)/shard_map/ppermute | solution.py:21
  232.9 6.1 collective-permute-start.31
  234.2 6.2 collective-permute-start.32
  271.9 6.8 %collective-permute-start.33 = (f32[1,16,256]{2,1,0:T(8,128)S(1)}, f32[1,16,256]{2,1,0:T(8,128)S(1)}, u32[]{:S(2)}, u32[]{:S(2)}) collective-permute-start(f32[1,16,256]{2,1,0:T(8,128)S(1)} %get-tuple-element.166), channel_id=1, source_target_pairs={{4,0},{8,4},{12,8},{5,1},{9,5},{13,9},{6,2},{10,6},{14,10},{7,3},{... | collective-permute-start | bytes 49160 | tf_op jit(solution)/shard_map/ppermute | solution.py:21
  278.7 6.1 collective-permute-start.35
  280.0 6.2 collective-permute-start.36
  315.1 11.3 %collective-permute-start.43 = (f32[1,16,256]{2,1,0:T(8,128)S(1)}, f32[1,16,256]{2,1,0:T(8,128)S(1)}, u32[]{:S(2)}, u32[]{:S(2)}) collective-permute-start(f32[1,16,256]{2,1,0:T(8,128)S(1)} %get-tuple-element.161), channel_id=1, source_target_pairs={{0,4},{4,8},{8,12},{1,5},{5,9},{9,13},{2,6},{6,10},{10,14},{3,7},{... | collective-permute-start | bytes 49160 | tf_op jit(solution)/shard_map/ppermute | solution.py:19
  316.7 9.7 %collective-permute-start.42 = (f32[1,16,256]{2,1,0:T(8,128)S(1)}, f32[1,16,256]{2,1,0:T(8,128)S(1)}, u32[]{:S(2)}, u32[]{:S(2)}) collective-permute-start(f32[1,16,256]{2,1,0:T(8,128)S(1)} %get-tuple-element.162), channel_id=1, source_target_pairs={{4,0},{8,4},{12,8},{5,1},{9,5},{13,9},{6,2},{10,6},{14,10},{7,3},{... | collective-permute-start | bytes 49160 | tf_op jit(solution)/shard_map/ppermute | solution.py:21
  319.2 13.1 %collective-permute-start.39 = (f32[1,16,256]{2,1,0:T(8,128)S(1)}, f32[1,16,256]{2,1,0:T(8,128)S(1)}, u32[]{:S(2)}, u32[]{:S(2)}) collective-permute-start(f32[1,16,256]{2,1,0:T(8,128)S(1)} %get-tuple-element.159), channel_id=1, source_target_pairs={{0,4},{4,8},{8,12},{1,5},{5,9},{9,13},{2,6},{6,10},{10,14},{3,7},{... | collective-permute-start | bytes 49160 | tf_op jit(solution)/shard_map/ppermute | solution.py:19
  324.9 7.4 %collective-permute-start.38 = (f32[1,16,256]{2,1,0:T(8,128)S(1)}, f32[1,16,256]{2,1,0:T(8,128)S(1)}, u32[]{:S(2)}, u32[]{:S(2)}) collective-permute-start(f32[1,16,256]{2,1,0:T(8,128)S(1)} %get-tuple-element.160), channel_id=1, source_target_pairs={{4,0},{8,4},{12,8},{5,1},{9,5},{13,9},{6,2},{10,6},{14,10},{7,3},{... | collective-permute-start | bytes 49160 | tf_op jit(solution)/shard_map/ppermute | solution.py:21
  326.5 12.2 %collective-permute-start.44 = (f32[34,1,256]{2,1,0:T(1,128)S(1)}, f32[34,1,256]{2,1,0:T(1,128)S(1)}, u32[]{:S(2)}, u32[]{:S(2)}) collective-permute-start(f32[34,1,256]{2,1,0:T(1,128)S(1)} %get-tuple-element.103), channel_id=1, source_target_pairs={{1,0},{2,1},{3,2},{5,4},{6,5},{7,6},{9,8},{10,9},{11,10},{13,12},{... | collective-permute-start | bytes 104456 | tf_op jit(solution)/shard_map/ppermute | solution.py:21
  327.8 10.9 %collective-permute-start.45 = (f32[34,1,256]{2,1,0:T(1,128)S(1)}, f32[34,1,256]{2,1,0:T(1,128)S(1)}, u32[]{:S(2)}, u32[]{:S(2)}) collective-permute-start(f32[34,1,256]{2,1,0:T(1,128)S(1)} %get-tuple-element.104), channel_id=1, source_target_pairs={{0,1},{1,2},{2,3},{4,5},{5,6},{6,7},{8,9},{9,10},{10,11},{12,13},{... | collective-permute-start | bytes 104456 | tf_op jit(solution)/shard_map/ppermute | solution.py:19
  332.4 6.2 collective-permute-start.40
  333.7 6.3 collective-permute-start.41
  340.8 6.9 %collective-permute-start.47 = (f32[1,16,256]{2,1,0:T(8,128)S(1)}, f32[1,16,256]{2,1,0:T(8,128)S(1)}, u32[]{:S(2)}, u32[]{:S(2)}) collective-permute-start(f32[1,16,256]{2,1,0:T(8,128)S(1)} %get-tuple-element.151), channel_id=1, source_target_pairs={{0,4},{4,8},{8,12},{1,5},{5,9},{9,13},{2,6},{6,10},{10,14},{3,7},{... | collective-permute-start | bytes 49160 | tf_op jit(solution)/shard_map/ppermute | solution.py:19
  346.3 6.5 %collective-permute-start.46 = (f32[1,16,256]{2,1,0:T(8,128)S(1)}, f32[1,16,256]{2,1,0:T(8,128)S(1)}, u32[]{:S(2)}, u32[]{:S(2)}) collective-permute-start(f32[1,16,256]{2,1,0:T(8,128)S(1)} %get-tuple-element.152), channel_id=1, source_target_pairs={{4,0},{8,4},{12,8},{5,1},{9,5},{13,9},{6,2},{10,6},{14,10},{7,3},{... | collective-permute-start | bytes 49160 | tf_op jit(solution)/shard_map/ppermute | solution.py:21
  352.8 6.4 %collective-permute-start.48 = (f32[34,1,256]{2,1,0:T(1,128)S(1)}, f32[34,1,256]{2,1,0:T(1,128)S(1)}, u32[]{:S(2)}, u32[]{:S(2)}) collective-permute-start(f32[34,1,256]{2,1,0:T(1,128)S(1)} %get-tuple-element.99), channel_id=1, source_target_pairs={{1,0},{2,1},{3,2},{5,4},{6,5},{7,6},{9,8},{10,9},{11,10},{13,12},{... | collective-permute-start | bytes 104456 | tf_op jit(solution)/shard_map/ppermute | solution.py:21
  354.1 6.5 %collective-permute-start.49 = (f32[34,1,256]{2,1,0:T(1,128)S(1)}, f32[34,1,256]{2,1,0:T(1,128)S(1)}, u32[]{:S(2)}, u32[]{:S(2)}) collective-permute-start(f32[34,1,256]{2,1,0:T(1,128)S(1)} %get-tuple-element.100), channel_id=1, source_target_pairs={{0,1},{1,2},{2,3},{4,5},{5,6},{6,7},{8,9},{9,10},{10,11},{12,13},{... | collective-permute-start | bytes 104456 | tf_op jit(solution)/shard_map/ppermute | solution.py:19
  388.0 6.8 %collective-permute-start.50 = (f32[1,16,256]{2,1,0:T(8,128)S(1)}, f32[1,16,256]{2,1,0:T(8,128)S(1)}, u32[]{:S(2)}, u32[]{:S(2)}) collective-permute-start(f32[1,16,256]{2,1,0:T(8,128)S(1)} %get-tuple-element.148), channel_id=1, source_target_pairs={{4,0},{8,4},{12,8},{5,1},{9,5},{13,9},{6,2},{10,6},{14,10},{7,3},{... | collective-permute-start | bytes 49160 | tf_op jit(solution)/shard_map/ppermute | solution.py:21
  394.9 6.1 collective-permute-start.52
  396.1 6.2 collective-permute-start.53
  433.8 6.8 %collective-permute-start.54 = (f32[1,16,256]{2,1,0:T(8,128)S(1)}, f32[1,16,256]{2,1,0:T(8,128)S(1)}, u32[]{:S(2)}, u32[]{:S(2)}) collective-permute-start(f32[1,16,256]{2,1,0:T(8,128)S(1)} %get-tuple-element.146), channel_id=1, source_target_pairs={{4,0},{8,4},{12,8},{5,1},{9,5},{13,9},{6,2},{10,6},{14,10},{7,3},{... | collective-permute-start | bytes 49160 | tf_op jit(solution)/shard_map/ppermute | solution.py:21
  440.6 6.1 collective-permute-start.56
  441.9 6.2 collective-permute-start.57
  477.0 10.5 %collective-permute-start.64 = (f32[1,16,256]{2,1,0:T(8,128)S(1)}, f32[1,16,256]{2,1,0:T(8,128)S(1)}, u32[]{:S(2)}, u32[]{:S(2)}) collective-permute-start(f32[1,16,256]{2,1,0:T(8,128)S(1)} %get-tuple-element.141), channel_id=1, source_target_pairs={{0,4},{4,8},{8,12},{1,5},{5,9},{9,13},{2,6},{6,10},{10,14},{3,7},{... | collective-permute-start | bytes 49160 | tf_op jit(solution)/shard_map/ppermute | solution.py:19
  478.6 8.8 %collective-permute-start.63 = (f32[1,16,256]{2,1,0:T(8,128)S(1)}, f32[1,16,256]{2,1,0:T(8,128)S(1)}, u32[]{:S(2)}, u32[]{:S(2)}) collective-permute-start(f32[1,16,256]{2,1,0:T(8,128)S(1)} %get-tuple-element.142), channel_id=1, source_target_pairs={{4,0},{8,4},{12,8},{5,1},{9,5},{13,9},{6,2},{10,6},{14,10},{7,3},{... | collective-permute-start | bytes 49160 | tf_op jit(solution)/shard_map/ppermute | solution.py:21
  480.4 13.0 %collective-permute-start.60 = (f32[1,16,256]{2,1,0:T(8,128)S(1)}, f32[1,16,256]{2,1,0:T(8,128)S(1)}, u32[]{:S(2)}, u32[]{:S(2)}) collective-permute-start(f32[1,16,256]{2,1,0:T(8,128)S(1)} %get-tuple-element.139), channel_id=1, source_target_pairs={{0,4},{4,8},{8,12},{1,5},{5,9},{9,13},{2,6},{6,10},{10,14},{3,7},{... | collective-permute-start | bytes 49160 | tf_op jit(solution)/shard_map/ppermute | solution.py:19
  486.1 7.2 %collective-permute-start.59 = (f32[1,16,256]{2,1,0:T(8,128)S(1)}, f32[1,16,256]{2,1,0:T(8,128)S(1)}, u32[]{:S(2)}, u32[]{:S(2)}) collective-permute-start(f32[1,16,256]{2,1,0:T(8,128)S(1)} %get-tuple-element.140), channel_id=1, source_target_pairs={{4,0},{8,4},{12,8},{5,1},{9,5},{13,9},{6,2},{10,6},{14,10},{7,3},{... | collective-permute-start | bytes 49160 | tf_op jit(solution)/shard_map/ppermute | solution.py:21
  487.5 12.2 %collective-permute-start.65 = (f32[34,1,256]{2,1,0:T(1,128)S(1)}, f32[34,1,256]{2,1,0:T(1,128)S(1)}, u32[]{:S(2)}, u32[]{:S(2)}) collective-permute-start(f32[34,1,256]{2,1,0:T(1,128)S(1)} %get-tuple-element.93), channel_id=1, source_target_pairs={{1,0},{2,1},{3,2},{5,4},{6,5},{7,6},{9,8},{10,9},{11,10},{13,12},{... | collective-permute-start | bytes 104456 | tf_op jit(solution)/shard_map/ppermute | solution.py:21
  488.8 10.9 %collective-permute-start.66 = (f32[34,1,256]{2,1,0:T(1,128)S(1)}, f32[34,1,256]{2,1,0:T(1,128)S(1)}, u32[]{:S(2)}, u32[]{:S(2)}) collective-permute-start(f32[34,1,256]{2,1,0:T(1,128)S(1)} %get-tuple-element.94), channel_id=1, source_target_pairs={{0,1},{1,2},{2,3},{4,5},{5,6},{6,7},{8,9},{9,10},{10,11},{12,13},{... | collective-permute-start | bytes 104456 | tf_op jit(solution)/shard_map/ppermute | solution.py:19
  493.4 6.2 collective-permute-start.61
  494.7 6.3 collective-permute-start.62
  501.8 6.9 %collective-permute-start.68 = (f32[1,16,256]{2,1,0:T(8,128)S(1)}, f32[1,16,256]{2,1,0:T(8,128)S(1)}, u32[]{:S(2)}, u32[]{:S(2)}) collective-permute-start(f32[1,16,256]{2,1,0:T(8,128)S(1)} %get-tuple-element.131), channel_id=1, source_target_pairs={{0,4},{4,8},{8,12},{1,5},{5,9},{9,13},{2,6},{6,10},{10,14},{3,7},{... | collective-permute-start | bytes 49160 | tf_op jit(solution)/shard_map/ppermute | solution.py:19
  507.3 6.5 %collective-permute-start.67 = (f32[1,16,256]{2,1,0:T(8,128)S(1)}, f32[1,16,256]{2,1,0:T(8,128)S(1)}, u32[]{:S(2)}, u32[]{:S(2)}) collective-permute-start(f32[1,16,256]{2,1,0:T(8,128)S(1)} %get-tuple-element.132), channel_id=1, source_target_pairs={{4,0},{8,4},{12,8},{5,1},{9,5},{13,9},{6,2},{10,6},{14,10},{7,3},{... | collective-permute-start | bytes 49160 | tf_op jit(solution)/shard_map/ppermute | solution.py:21
  513.9 6.4 %collective-permute-start.69 = (f32[34,1,256]{2,1,0:T(1,128)S(1)}, f32[34,1,256]{2,1,0:T(1,128)S(1)}, u32[]{:S(2)}, u32[]{:S(2)}) collective-permute-start(f32[34,1,256]{2,1,0:T(1,128)S(1)} %get-tuple-element.89), channel_id=1, source_target_pairs={{1,0},{2,1},{3,2},{5,4},{6,5},{7,6},{9,8},{10,9},{11,10},{13,12},{... | collective-permute-start | bytes 104456 | tf_op jit(solution)/shard_map/ppermute | solution.py:21
  515.2 6.5 %collective-permute-start.70 = (f32[34,1,256]{2,1,0:T(1,128)S(1)}, f32[34,1,256]{2,1,0:T(1,128)S(1)}, u32[]{:S(2)}, u32[]{:S(2)}) collective-permute-start(f32[34,1,256]{2,1,0:T(1,128)S(1)} %get-tuple-element.90), channel_id=1, source_target_pairs={{0,1},{1,2},{2,3},{4,5},{5,6},{6,7},{8,9},{9,10},{10,11},{12,13},{... | collective-permute-start | bytes 104456 | tf_op jit(solution)/shard_map/ppermute | solution.py:19
  548.9 6.8 %collective-permute-start.71 = (f32[1,16,256]{2,1,0:T(8,128)S(1)}, f32[1,16,256]{2,1,0:T(8,128)S(1)}, u32[]{:S(2)}, u32[]{:S(2)}) collective-permute-start(f32[1,16,256]{2,1,0:T(8,128)S(1)} %get-tuple-element.128), channel_id=1, source_target_pairs={{4,0},{8,4},{12,8},{5,1},{9,5},{13,9},{6,2},{10,6},{14,10},{7,3},{... | collective-permute-start | bytes 49160 | tf_op jit(solution)/shard_map/ppermute | solution.py:21
  555.8 6.1 collective-permute-start.73
  557.1 6.2 collective-permute-start.74
  594.7 6.8 %collective-permute-start.75 = (f32[1,16,256]{2,1,0:T(8,128)S(1)}, f32[1,16,256]{2,1,0:T(8,128)S(1)}, u32[]{:S(2)}, u32[]{:S(2)}) collective-permute-start(f32[1,16,256]{2,1,0:T(8,128)S(1)} %get-tuple-element.126), channel_id=1, source_target_pairs={{4,0},{8,4},{12,8},{5,1},{9,5},{13,9},{6,2},{10,6},{14,10},{7,3},{... | collective-permute-start | bytes 49160 | tf_op jit(solution)/shard_map/ppermute | solution.py:21
  601.5 6.1 collective-permute-start.77
  602.8 6.2 collective-permute-start.78
  (25 other events, 108.9 us)
